TPU v7x, 32 devices: a whole 2x2x4 slice. The times are simulated.
32 devices in a mesh: gx: 8 (over z, y), gy: 4 (over x, core).
Axes of the slice: x: 2, y: 2, z: 4, core: 2. Of those that a mesh axis runs over, the one named last changes fastest.
Arguments:
- hidden: bfloat16 [4096, 14336], P('gx', 'gy'), may hold values from -6 to 6
- weight: bfloat16 [4096, 14336], P(None, 'gy'), may hold values from -0.0625 to 0.0625
- cotangent: bfloat16 [4096, 4096], P('gx', 'gy'), may hold values from -6 to 6
Outputs:
- output: bfloat16 [4096, 4096], P('gx', 'gy')
- hidden_grad: bfloat16 [4096, 14336], P('gx', 'gy')
- weight_grad: float32 [4096, 14336], P('gx', 'gy')
All inputs are finite; a program needn't handle non-finite values.
Results may differ from a plain program's by a relative error of at most 0.001.
Values may be sent and summed in bfloat16 or wider, within the bound.
A program may use at most 128 MiB of HBM per device.

v0:
```python
import jax
import jax.numpy as jnp
from jax import lax
from jax.sharding import PartitionSpec as P


def shards(hidden, weight, cotangent):
    tok_rows = hidden.shape[0]
    grad_scale = float(tok_rows * lax.axis_size("gx")) ** (-0.5)
    output_rows = lax.psum_scatter(
        lax.dot_general(
            weight, hidden, (((1,), (1,)), ((), ())), preferred_element_type=jnp.float32
        ),
        "gy",
        scatter_dimension=0,
        tiled=True,
    )
    output = output_rows.T.astype(jnp.bfloat16)
    cotangent_full = lax.all_gather(cotangent, "gy", axis=1, tiled=True)
    hidden_grad = jnp.dot(cotangent_full, weight, preferred_element_type=jnp.float32).astype(
        jnp.bfloat16
    )
    own_blocks = lax.all_to_all(cotangent_full, "gx", split_axis=1, concat_axis=0, tiled=True)
    summed = lax.dot_general(
        own_blocks,
        lax.all_gather(hidden, "gx", axis=0, tiled=True),
        (((0,), (0,)), ((), ())),
        preferred_element_type=jnp.float32,
    )
    weight_grad = summed * grad_scale
    return (output, hidden_grad, weight_grad)


def solution(mesh):
    return jax.shard_map(
        shards,
        mesh=mesh,
        in_specs=(P("gx", "gy"), P(None, "gy"), P("gx", "gy")),
        out_specs=(P("gx", "gy"), P("gx", "gy"), P("gx", "gy")),
        check_vma=False,
    )
```

profile of v0, /device:TPU:5, one launch (start us, length us, event | category | flops | bytes accessed | tf_op | source)
XLA Modules:
  0.0 715.4 jit_solution(5855176551937631784)
XLA Ops:
  7.2 0.0 all-gather.3.cloned.1.call-start
  7.2 2.3 copy.8
  9.5 0.0 all-gather.3.cloned.1.call-update
  9.5 0.0 reduce-scatter.2.cloned.1.call-start
  9.6 22.4 %fusion = f32[4096,512]{1,0:T(8,128)} fusion(bf16[4096,3584]{1,0:T(8,128)(2,1)} %param.4, bf16[512,3584]{1,0:T(8,128)(2,1)} %param.3), kind=kOutput, calls=%fused_computation.3 | convolution fusion | flops 15032385536 | bytes 41418752 | tf_op jit(solution)/shard_map/dot_general | solution.py:11
  32.0 0.0 reduce-scatter.2.cloned.1.call-update
  32.0 0.0 all-gather.5.cloned.1.call-start
  32.0 0.7 all-gather.5.cloned.1.call-update
  32.7 13.5 %all-gather.3.cloned.1.call-done = bf16[512,4096]{0,1:T(8,128)(2,1)} async-done(((bf16[512,1024]{0,1:T(8,128)(2,1)}), bf16[512,4096]{0,1:T(8,128)(2,1)}) %all-gather.3.cloned.1.call-update) | async-done | bytes 4194320 | tf_op jit(solution)/shard_map/all_gather | solution.py:19
  46.2 5.5 all-to-all-start
  51.7 25.7 %convolution_convert_fusion = bf16[512,3584]{1,0:T(8,128)(2,1)} fusion(bf16[512,4096]{0,1:T(8,128)(2,1)} %all-gather.3.cloned.1.call-done, bf16[4096,3584]{1,0:T(8,128)(2,1)} %param.4), kind=kOutput, calls=%fused_computation.1 | convolution fusion | flops 15034220544 | bytes 37224448 | tf_op jit(solution)/shard_map/dot_general | solution.py:20
  77.4 107.6 %all-to-all-done = bf16[512,8,512]{0,2,1:T(8,128)(2,1)} async-done(((bf16[512,8,512]{0,2,1:T(8,128)(2,1)}), bf16[512,8,512]{0,2,1:T(8,128)(2,1)}, u32[]{:S(2)}, u32[]{:S(2)}) %all-to-all-start) | async-done | bytes 4194336 | tf_op jit(solution)/shard_map/all_to_all | solution.py:23
  185.0 6.5 copy.9
  191.5 0.0 reduce-scatter.2.cloned.1.call-done
  191.5 1.7 convert_bitcast_fusion
  193.2 1.3 copy.10
  194.5 490.4 %all-gather.5.cloned.1.call-done = bf16[4096,3584]{1,0:T(8,128)(2,1)} async-done(((bf16[512,3584]{1,0:T(8,128)(2,1)}), bf16[4096,3584]{1,0:T(8,128)(2,1)}) %all-gather.5.cloned.1.call-update) | async-done | bytes 29360144 | tf_op jit(solution)/shard_map/all_gather | solution.py:26
  684.9 23.9 %convolution_multiply_fusion = f32[512,3584]{1,0:T(8,128)} fusion(bf16[4096,512]{1,0:T(8,128)(2,1)} %bitcast.12, bf16[4096,3584]{1,0:T(8,128)(2,1)} %all-gather.5.cloned.1.call-done), kind=kOutput, calls=%fused_computation | convolution fusion | flops 15034220544 | bytes 40894464 | tf_op jit(solution)/shard_map/dot_general | solution.py:24
Async XLA Ops:
  7.2 39.0 %all-gather.3.cloned.1.call-start = ((), (), s32[]{:S(2)}) async-start(), calls=%async_computation.3 | async-start | bytes 5242880 | tf_op jit(solution)/shard_map/all_gather | solution.py:19
  9.5 182.0 %reduce-scatter.2.cloned.1.call-start = ((), (), s32[]{:S(2)}) async-start(), calls=%async_computation.2 | async-start | bytes 10485760 | tf_op jit(solution)/shard_map/reduce_scatter | solution.py:10
  32.0 653.0 %all-gather.5.cloned.1.call-start = ((), (), s32[]{:S(2)}) async-start(), calls=%async_computation.4 | async-start | bytes 33030144 | tf_op jit(solution)/shard_map/all_gather | solution.py:26
  46.2 138.8 %all-to-all-start = ((bf16[512,8,512]{0,2,1:T(8,128)(2,1)}), bf16[512,8,512]{0,2,1:T(8,128)(2,1)}, u32[]{:S(2)}, u32[]{:S(2)}) async-start(bf16[512,8,512]{0,2,1:T(8,128)(2,1)} %bitcast.11), calls=%async_computation.1 | async-start | bytes 8388608 | tf_op jit(solution)/shard_map/all_to_all | solution.py:23
Sparse Core Ops, SparseCore 0:
  10.1 36.0 all-gather.2
  48.8 70.8 reduce-scatter.1
  121.2 563.7 all-gather.4
where the time goes:
time: 716 us; the launch traced here: 715 us
  waiting for transfers between devices  612 us (85%)
  matrix products  72 us (10%)
  between operations  13.7 us (2%)
  local copies, waits for them, and re-layouts  10.1 us (1%)
    all_gather x1, waiting for transfers between devices, shards(): lax.all_gather(hidden, 'gx', axis=0, tiled=True)  490 us
    all_to_all x1, waiting for transfers between devices, shards(): lax.all_to_all(cotangent_full, 'gx', split_axis=1, concat_axis=0, tiled=T...  108 us
    dot_general x1, matrix products, shards(): jnp.dot(cotangent_full, weight, preferred_element_type=jnp.float32)  25.7 us
    dot_general x1, matrix products, shards(): lax.dot_general(own_blocks, lax.all_gather(hidden, 'gx', axis=0, tiled=Tr...  23.9 us
    dot_general x1, matrix products, shards(): lax.dot_general(weight, hidden, (((1,), (1,)), ((), ())), preferred_eleme...  22.4 us
  transfers between devices with their start and end apart: 4, of which 3 were waited for; matrix products, arithmetic and copies ran while one was open for 8% of the time, Pallas kernels for 0%

commit v1 on v0

--- a/solution.py
+++ b/solution.py
@@ -2,6 +2,7 @@
 import jax.numpy as jnp
 from jax import lax
 from jax.sharding import PartitionSpec as P
+from jax.lax import all_to_all, axis_size
 
 
 def shards(hidden, weight, cotangent):
@@ -20,7 +21,10 @@
     hidden_grad = jnp.dot(cotangent_full, weight, preferred_element_type=jnp.float32).astype(
         jnp.bfloat16
     )
-    own_blocks = lax.all_to_all(cotangent_full, "gx", split_axis=1, concat_axis=0, tiled=True)
+    fix_windows = lambda z_in: jnp.concatenate(
+        all_to_all(jnp.stack(jnp.split(z_in, axis_size("gx"), 1)), "gx", 0, 0), 0
+    )
+    own_blocks = fix_windows(cotangent_full)
     summed = lax.dot_general(
         own_blocks,
         lax.all_gather(hidden, "gx", axis=0, tiled=True),

time: 716 us -> 721 us (level)
    reduce_scatter x1, waiting for transfers between devices: 0.01 us -> 28.9 us  [shards(): lax.psum_scatter(lax.dot_general(weight, hidden, (((1,), (1,)), ((), ()))...]
    all_to_all x1, waiting for transfers between devices: 108 us -> 83.8 us  [shards(): all_to_all(jnp.stack(jnp.split(z_in, axis_size('gx'), 1)), 'gx', 0, 0)]
    unnamed x2 -> x8, local copies, waits for them, and re-layouts: 3.59 us -> 14.7 us
    all_gather x1, waiting for transfers between devices: 490 us -> 483 us  [shards(): lax.all_gather(hidden, 'gx', axis=0, tiled=True)]
  transfers between devices with their start and end apart: 4 -> 4, of which waited for: 3 -> 4; matrix products, arithmetic and copies ran while one was open for 8% -> 9% of each run, Pallas kernels for 0% -> 0%
where the time goes in v1:
time: 721 us; the launch traced here: 719 us
  waiting for transfers between devices  611 us (85%)
  matrix products  70.2 us (10%)
  local copies, waits for them, and re-layouts  16.6 us (2%)
  between operations  13.8 us (2%)
    all_gather x1, waiting for transfers between devices, shards(): lax.all_gather(hidden, 'gx', axis=0, tiled=True)  483 us
    all_to_all x1, waiting for transfers between devices, shards(): all_to_all(jnp.stack(jnp.split(z_in, axis_size('gx'), 1)), 'gx', 0, 0)  83.8 us
    reduce_scatter x1, waiting for transfers between devices, shards(): lax.psum_scatter(lax.dot_general(weight, hidden, (((1,), (1,)), ((), ()))...  28.9 us
    dot_general x1, matrix products, shards(): lax.dot_general(own_blocks, lax.all_gather(hidden, 'gx', axis=0, tiled=Tr...  23.9 us
    dot_general x1, matrix products, shards(): jnp.dot(cotangent_full, weight, preferred_element_type=jnp.float32)  23.8 us
    dot_general x1, matrix products, shards(): lax.dot_general(weight, hidden, (((1,), (1,)), ((), ())), preferred_eleme...  22.5 us
    unnamed x8, local copies, waits for them, and re-layouts  14.7 us
  transfers between devices with their start and end apart: 4, of which 4 were waited for; matrix products, arithmetic and copies ran while one was open for 9% of the time, Pallas kernels for 0%

profile of v1, /device:TPU:5, one launch (start us, length us, event | category | flops | bytes accessed | tf_op | source)
XLA Modules:
  0.0 719.4 jit_solution(5019832398603892576)
XLA Ops:
  7.2 0.0 all-gather.3.cloned.1.call-start
  7.2 0.7 all-gather.3.cloned.1.call-update
  7.9 0.0 reduce-scatter.2.cloned.1.call-start
  7.9 22.5 %fusion.8 = f32[4096,512]{1,0:T(8,128)} fusion(bf16[4096,3584]{1,0:T(8,128)(2,1)} %param.4, bf16[512,3584]{1,0:T(8,128)(2,1)} %param.3), kind=kOutput, calls=%fused_computation.19 | convolution fusion | flops 15032385536 | bytes 41418752 | tf_op jit(solution)/shard_map/dot_general | solution.py:12
  30.5 0.0 reduce-scatter.2.cloned.1.call-update
  30.5 0.0 all-gather.5.cloned.1.call-start
  30.6 0.7 all-gather.5.cloned.1.call-update
  31.3 14.4 %all-gather.3.cloned.1.call-done = bf16[512,4096]{1,0:T(8,128)(2,1)} async-done(((bf16[512,1024]{1,0:T(8,128)(2,1)}), bf16[512,4096]{1,0:T(8,128)(2,1)}) %all-gather.3.cloned.1.call-update) | async-done | bytes 4194320 | tf_op jit(solution)/shard_map/all_gather | solution.py:20
  45.6 1.9 fusion.7
  47.5 1.9 fusion.6
  49.4 1.9 fusion.5
  51.2 1.9 fusion.4
  53.1 2.0 fusion.3
  55.1 1.9 fusion.2
  57.0 2.0 fusion.1
  59.0 2.0 fusion
  61.0 5.5 all-to-all-start
  66.5 23.8 %convolution_convert_fusion = bf16[512,3584]{1,0:T(8,128)(2,1)} fusion(bf16[512,4096]{1,0:T(8,128)(2,1)} %all-gather.3.cloned.1.call-done, bf16[4096,3584]{1,0:T(8,128)(2,1)} %param.4), kind=kOutput, calls=%fused_computation.1 | convolution fusion | flops 15034220544 | bytes 37224448 | tf_op jit(solution)/shard_map/dot_general | solution.py:21
  90.2 28.9 %reduce-scatter.2.cloned.1.call-done = f32[1024,512]{1,0:T(8,128)} async-done(((f32[4096,512]{1,0:T(8,128)}), f32[1024,512]{1,0:T(8,128)}) %reduce-scatter.2.cloned.1.call-update) | async-done | bytes 2097168 | tf_op jit(solution)/shard_map/reduce_scatter | solution.py:11
  119.1 1.7 convert_bitcast_fusion
  120.8 1.3 copy.6
  122.1 83.8 %all-to-all-done = bf16[8,512,512]{2,1,0:T(8,128)(2,1)} async-done(((bf16[8,512,512]{2,1,0:T(8,128)(2,1)}), bf16[8,512,512]{2,1,0:T(8,128)(2,1)}, u32[]{:S(2)}, u32[]{:S(2)}) %all-to-all-start) | async-done | bytes 4194336 | tf_op jit(solution)/shard_map/all_to_all | solution.py:25
  205.9 483.0 %all-gather.5.cloned.1.call-done = bf16[4096,3584]{1,0:T(8,128)(2,1)} async-done(((bf16[512,3584]{1,0:T(8,128)(2,1)}), bf16[4096,3584]{1,0:T(8,128)(2,1)}) %all-gather.5.cloned.1.call-update) | async-done | bytes 29360144 | tf_op jit(solution)/shard_map/all_gather | solution.py:30
  689.0 23.9 %convolution_multiply_fusion = f32[512,3584]{1,0:T(8,128)} fusion(bf16[4096,512]{1,0:T(8,128)(2,1)} %bitcast.9, bf16[4096,3584]{1,0:T(8,128)(2,1)} %all-gather.5.cloned.1.call-done), kind=kOutput, calls=%fused_computation | convolution fusion | flops 15034220544 | bytes 40894464 | tf_op jit(solution)/shard_map/dot_general | solution.py:28
Async XLA Ops:
  7.2 38.5 %all-gather.3.cloned.1.call-start = ((), (), s32[]{:S(2)}) async-start(), calls=%async_computation.3 | async-start | bytes 5242880 | tf_op jit(solution)/shard_map/all_gather | solution.py:20
  7.9 111.2 %reduce-scatter.2.cloned.1.call-start = ((), (), s32[]{:S(2)}) async-start(), calls=%async_computation.2 | async-start | bytes 10485760 | tf_op jit(solution)/shard_map/reduce_scatter | solution.py:11
  30.5 658.4 %all-gather.5.cloned.1.call-start = ((), (), s32[]{:S(2)}) async-start(), calls=%async_computation.4 | async-start | bytes 33030144 | tf_op jit(solution)/shard_map/all_gather | solution.py:30
  61.0 145.0 %all-to-all-start = ((bf16[8,512,512]{2,1,0:T(8,128)(2,1)}), bf16[8,512,512]{2,1,0:T(8,128)(2,1)}, u32[]{:S(2)}, u32[]{:S(2)}) async-start(bf16[8,512,512]{2,1,0:T(8,128)(2,1)} %fusion), calls=%async_computation.1 | async-start | bytes 8388608 | tf_op jit(solution)/shard_map/all_to_all | solution.py:25
Sparse Core Ops, SparseCore 0:
  9.5 36.0 all-gather.2
  48.2 70.8 reduce-scatter.1
  120.6 568.2 all-gather.4
